TPU v7x, 8 devices: a whole 2x2x1 slice. The times are simulated.
8 devices in a mesh: rep: 2 (over z, y), dp: 4 (over x, core).
Axes of the slice: x: 2, y: 2, z: 1, core: 2. Of those that a mesh axis runs over, the one named last changes fastest.
Arguments:
- hidden: bfloat16 [512, 7168], P(('rep', 'dp')), parts along dimension 0
- ckv_cache: bfloat16 [512, 512, 512], P(('rep', 'dp')), parts along dimension 0
- kpe_cache: bfloat16 [512, 512, 64], P(('rep', 'dp')), parts along dimension 0
- cache_len: int32 [512], P(('rep', 'dp')), parts along dimension 0
- rope_cos: float32 [512, 32], P(('rep', 'dp')), parts along dimension 0
- rope_sin: float32 [512, 32], P(('rep', 'dp')), parts along dimension 0
- norm_attn: float32 [7168], replicated
- w_dq: bfloat16 [7168, 1536], replicated
- norm_q: float32 [1536], replicated
- w_uq: bfloat16 [1536, 64, 192], replicated
- w_dkv: bfloat16 [7168, 576], replicated
- norm_kv: float32 [512], replicated
- w_uk: bfloat16 [512, 64, 128], replicated
- w_uv: bfloat16 [512, 64, 128], replicated
- w_out: bfloat16 [64, 128, 7168], replicated
- norm_mlp: float32 [7168], replicated
- w_gate: bfloat16 [7168, 18432], P(None, 'dp')
- w_up: bfloat16 [7168, 18432], P(None, 'dp')
- w_down: bfloat16 [18432, 7168], P('dp')
Outputs:
- output 1: bfloat16 [512, 7168], P(('rep', 'dp')), parts along dimension 0
- output 2: bfloat16 [512, 512], P(('rep', 'dp')), parts along dimension 0
- output 3: bfloat16 [512, 64], P(('rep', 'dp')), parts along dimension 0
There are 2 independent parts. A program takes and returns all parts, laid end to end along the dimension named above; an argument that names none is the same for every part.
All inputs are finite; a program needn't handle non-finite values.
Results may differ from a plain program's by a relative error of at most 0.0108563.
Values are sent between devices in bfloat16 or wider.
A program may use at most 1.75 GiB of HBM per device.

v0:
```python
import math
import jax
import jax.numpy as jnp
from jax import lax
from jax.sharding import PartitionSpec as P

EPSILON = 1e-6
MSCALE = 0.1 * math.log(40.0) + 1.0


def rms_norm(values_in, gain_vec):
    floats = values_in.astype(jnp.float32)
    mean_sq = jnp.mean(floats * floats, axis=-1, keepdims=True)
    return floats * lax.rsqrt(mean_sq + EPSILON) * gain_vec


def apply_rope(values_in, cos_t, sin_t):
    half_dim = values_in.shape[-1] // 2
    low_half = values_in[..., :half_dim]
    high_half = values_in[..., half_dim:]
    return jnp.concatenate([low_half * cos_t - high_half * sin_t, high_half * cos_t + low_half * sin_t], axis=-1)


def attention_rows(hidden, ckv_cache, kpe_cache, cache_len, rope_cos, rope_sin, norm_attn, w_dq, norm_q, w_uq, w_dkv, norm_kv, w_uk, w_uv, w_out):
    nope_dim = w_uk.shape[2]
    value_a7 = w_uk.shape[0]
    score_scale = MSCALE * MSCALE / math.sqrt(w_uq.shape[2])
    normed = rms_norm(hidden, norm_attn).astype(jnp.bfloat16)
    q_latent = rms_norm(jnp.dot(normed, w_dq, preferred_element_type=jnp.float32), norm_q).astype(jnp.bfloat16)
    q_full = jnp.einsum('bl,lhe->bhe', q_latent, w_uq, preferred_element_type=jnp.float32)
    q_nope = q_full[..., :nope_dim].astype(jnp.bfloat16)
    q_pe = apply_rope(q_full[..., nope_dim:], rope_cos[:, None, :], rope_sin[:, None, :]).astype(jnp.bfloat16)
    kv_full = jnp.dot(normed, w_dkv, preferred_element_type=jnp.float32)
    ckv_new = rms_norm(kv_full[:, :value_a7], norm_kv).astype(jnp.bfloat16)
    kpe_new = apply_rope(kv_full[:, value_a7:], rope_cos, rope_sin).astype(jnp.bfloat16)
    q_abs = jnp.einsum('bhn,lhn->bhl', q_nope, w_uk, preferred_element_type=jnp.float32).astype(jnp.bfloat16)
    scores = (jnp.einsum('bhl,btl->bht', q_abs, ckv_cache, preferred_element_type=jnp.float32)
              + jnp.einsum('bhr,btr->bht', q_pe, kpe_cache, preferred_element_type=jnp.float32)) * score_scale
    positions = jnp.arange(ckv_cache.shape[1])
    scores = jnp.where(positions[None, None, :] < cache_len[:, None, None], scores, -jnp.inf)
    score_new = (jnp.einsum('bhl,bl->bh', q_abs, ckv_new, preferred_element_type=jnp.float32)
                 + jnp.einsum('bhr,br->bh', q_pe, kpe_new, preferred_element_type=jnp.float32)) * score_scale
    row_max = jnp.maximum(jnp.max(scores, axis=-1), score_new)
    exp_cache = jnp.exp(scores - row_max[..., None])
    exp_new = jnp.exp(score_new - row_max)
    norm_sum = jnp.sum(exp_cache, axis=-1) + exp_new
    weighted = (jnp.einsum('bht,btl->bhl', exp_cache.astype(jnp.bfloat16), ckv_cache, preferred_element_type=jnp.float32)
                + exp_new.astype(jnp.bfloat16).astype(jnp.float32)[..., None] * ckv_new.astype(jnp.float32)[:, None, :])
    lat_out = (weighted / norm_sum[..., None]).astype(jnp.bfloat16)
    head_out = jnp.einsum('bhl,lhv->bhv', lat_out, w_uv, preferred_element_type=jnp.float32).astype(jnp.bfloat16)
    attn_out = jnp.einsum('bhv,hvd->bd', head_out, w_out, preferred_element_type=jnp.float32)
    residual = (hidden.astype(jnp.float32) + attn_out).astype(jnp.bfloat16)
    return residual, ckv_new, kpe_new


def solution(mesh):
    row_spec = P(('rep', 'dp'), None)
    cube_spec = P(('rep', 'dp'), None, None)
    full_spec = P()
    in_specs = (row_spec, cube_spec, cube_spec, P(('rep', 'dp')), row_spec, row_spec,
                full_spec, full_spec, full_spec, full_spec, full_spec, full_spec, full_spec, full_spec, full_spec, full_spec,
                P(None, 'dp'), P(None, 'dp'), P('dp', None))

    def local_step(hidden, ckv_cache, kpe_cache, cache_len, rope_cos, rope_sin, norm_attn, w_dq, norm_q, w_uq, w_dkv, norm_kv, w_uk, w_uv, w_out, norm_mlp, w_gate, w_up, w_down):
        residual, ckv_new, kpe_new = attention_rows(hidden, ckv_cache, kpe_cache, cache_len, rope_cos, rope_sin, norm_attn, w_dq, norm_q, w_uq, w_dkv, norm_kv, w_uk, w_uv, w_out)
        mlp_in = rms_norm(residual, norm_mlp).astype(jnp.bfloat16)
        group_in = lax.all_gather(mlp_in, 'dp', axis=0, tiled=True)
        gate_val = jnp.dot(group_in, w_gate, preferred_element_type=jnp.float32)
        up_val = jnp.dot(group_in, w_up, preferred_element_type=jnp.float32)
        act_val = (jax.nn.silu(gate_val) * up_val).astype(jnp.bfloat16)
        partial_sum = jnp.dot(act_val, w_down, preferred_element_type=jnp.float32)
        mlp_rows = lax.psum_scatter(partial_sum, 'dp', scatter_dimension=0, tiled=True)
        out_hidden = (residual.astype(jnp.float32) + mlp_rows).astype(jnp.bfloat16)
        return out_hidden, ckv_new, kpe_new

    return jax.shard_map(local_step, mesh=mesh, in_specs=in_specs, out_specs=(row_spec, row_spec, row_spec), check_vma=False)
```

profile of v0, /device:TPU:0, one launch (start us, length us, event | category | flops | bytes accessed | tf_op | source)
XLA Modules:
  0.0 382.3 jit_solution(17135390089911029604)
XLA Ops:
  7.2 0.0 all-gather.2.cloned.1.call-start
  7.2 1.5 fusion.27
  8.7 0.0 copy-start.12
  8.7 0.0 copy-start.7
  8.7 0.0 copy-start.6
  8.7 0.0 copy-start.2
  8.7 0.0 copy-start.4
  8.7 6.3 %fusion.48 = f32[64,576]{1,0:T(8,128)S(1)} fusion(bf16[7168,576]{0,1:T(8,128)(2,1)} %param.29, bf16[64,7168]{1,0:T(8,128)(2,1)} %param.19, f32[7168]{0:T(1024)} %param.25, f32[64]{0:T(128)S(1)} %add_rsqrt_fusion.3), kind=kOutput, calls=%fused_computation.48 | convolution fusion | flops 530317312 | bytes 9351424 | tf_op jit(solution)/shard_map/dot_general | solution.py:33
  15.0 0.1 multiply_reduce_fusion.2
  15.2 0.1 fusion.65
  15.2 0.0 copy-done.12
  15.2 0.1 iota_compare_fusion
  15.3 0.0 copy-done.7
  15.3 0.1 copy.33
  15.4 0.0 copy-done.6
  15.4 0.1 copy.34
  15.5 0.1 copy.46
  15.6 0.1 copy.45
  15.7 0.6 pad_maximum_fusion.1
  16.3 0.1 copy.41
  16.4 0.0 copy-done.2
  16.4 0.0 copy-done.4
  16.4 0.0 copy-start.10
  16.4 9.5 %multiply_reduce_fusion.1 = (f32[64]{0:T(128)S(1)}, f32[64,1536]{1,0:T(8,128)S(1)}) fusion(bf16[7168,1536]{1,0:T(8,128)(2,1)} %param.26, bf16[64,7168]{1,0:T(8,128)(2,1)S(1)} %copy-done.2, f32[7168]{0:T(1024)S(1)} %copy-done.4, f32[64]{0:T(128)S(1)} %add_rsqrt_fusion.3), kind=kOutput, calls=%fused_computation.47 | convolution fusion | flops 1411317760 | bytes 23360000 | tf_op jit(solution)/shard_map/dot_general | solution.py:29
  25.9 0.0 copy-done.10
  25.9 19.9 %fusion.53 = f32[64,64,192]{2,0,1:T(8,128)} fusion(bf16[1536,64,192]{0,2,1:T(8,128)(2,1)} %param.28, f32[64,1536]{1,0:T(8,128)S(1)} %get-tuple-element.19, f32[1536]{0:T(1024)S(1)} %copy-done.10, f32[64]{0:T(128)S(1)} %add_rsqrt_fusion.2), kind=kOutput, calls=%fused_computation.51 | convolution fusion | flops 2416214016 | bytes 41294080 | tf_op jit(solution)/shard_map/bl,lhe->bhe/dot_general | solution.py:30
  45.9 0.0 copy-start
  45.9 21.4 %convert_bitcast_fusion = bf16[64,64,512]{2,0,1:T(8,128)(2,1)S(1)} fusion(bf16[512,64,128]{2,1,0:T(8,128)(2,1)} %param.31, f32[64,64,192]{2,0,1:T(8,128)} %fusion.53), kind=kOutput, calls=%fused_computation.20 | convolution fusion | flops 538968064 | bytes 13631488 | tf_op jit(solution)/shard_map/bhn,lhn->bhl/dot_general | solution.py:36
  67.3 0.0 copy-done
  67.3 0.0 copy-start.1
  67.3 0.0 copy-start.3
  67.4 0.7 subtract_convert_fusion
  68.1 0.6 pad_maximum_fusion
  68.7 0.8 fusion.40
  69.5 1.5 copy-done.3
  71.0 0.0 copy-start.11
  71.1 4.6 %fusion.42 = f32[64,64,512]{2,1,0:T(8,128)} fusion(bf16[64,512,64]{1,2,0:T(8,128)(2,1)S(1)} %copy-done.3, bf16[64,64,64]{2,0,1:T(8,128)(2,1)S(1)} %pad_maximum_fusion), kind=kOutput, calls=%fused_computation.44 | convolution fusion | flops 268435456 | bytes 13107200 | tf_op jit(solution)/shard_map/bhr,btr->bht/dot_general | solution.py:38
  75.7 0.0 copy-done.11
  75.7 0.1 fusion.64
  75.8 0.0 copy-start.5
  75.8 0.0 copy-done.1
  75.8 0.6 copy-done.5
  76.4 2.3 fusion.17
  78.7 23.3 %fusion.14 = (f32[64,64]{1,0:T(8,128)S(1)}, f32[64,64,512]{2,1,0:T(8,128)}) fusion(f32[64,64,512]{2,1,0:T(8,128)} %fusion.42, pred[64,512]{1,0:T(8,128)(4,1)S(1)} %iota_compare_fusion, bf16[64,512,512]{2,1,0:T(8,128)(2,1)} %param.20, bf16[64,64,512]{2,0,1:T(8,128)(2,1)} %copy-done.1), kind=kOutput, calls=%fused_computation.18 | convolution fusion | flops 2155868160 | bytes 54575104 | tf_op jit(solution)/shard_map/bhl,btl->bht/dot_general | solution.py:37
  102.0 7.2 %fusion.7 = f32[64,64]{1,0:T(8,128)S(1)} fusion(f32[64,64]{1,0:T(8,128)S(1)} %fusion.58, f32[64,64,512]{2,1,0:T(8,128)} %get-tuple-element.21, f32[64,64,512]{2,1,0:T(8,128)} %fusion.42, pred[64,512]{1,0:T(8,128)(4,1)S(1)} %iota_compare_fusion), kind=kLoop, calls=%fused_computation.11 | loop fusion | flops 10481664 | bytes 16842752 | tf_op jit(solution)/shard_map/reduce_sum | solution.py:46
  109.2 18.5 %divide_convert_fusion = bf16[64,64,512]{2,1,0:T(8,128)(2,1)S(1)} fusion(f32[64,64]{1,0:T(8,128)S(1)} %get-tuple-element.13, f32[64,512]{1,0:T(8,128)S(1)} %get-tuple-element.6, f32[64,64]{1,0:T(8,128)S(1)} %get-tuple-element.12, bf16[64,512,512]{2,1,0:T(8,128)(2,1)} %param.20, f32[64,64]{1,0:T(8,128)S(1)} %fusion.58, f32[64,64,512]{2,1,0:T(8,128)} %get-tuple-element.21, ...), kind=kOutput, calls=%fused_computation.4 | convolution fusion | flops 2166358016 | bytes 54738944 | tf_op jit(solution)/shard_map/bht,btl->bhl/dot_general | solution.py:47
  127.7 24.3 %fusion.35.clone.1.clone.4 = bf16[64,64,128]{2,0,1:T(8,128)(2,1)} fusion(bf16[512,64,128]{2,1,0:T(8,128)(2,1)} %param.32, bf16[64,64,512]{2,1,0:T(8,128)(2,1)S(1)} %divide_convert_fusion), kind=kOutput, calls=%fused_computation.40.clone.clone.clone.clone.clone.1 | convolution fusion | flops 537395200 | bytes 13631488 | tf_op jit(solution)/shard_map/bhl,lhv->bhv/dot_general | solution.py:50
  152.1 0.0 copy-start.9
  152.1 38.7 %multiply_reduce_fusion = (f32[64]{0:T(128)S(1)}, f32[64,7168]{1,0:T(8,128)S(1)}) fusion(bf16[64,128,7168]{2,1,0:T(8,128)(2,1)} %param.33, bf16[64,7168]{1,0:T(8,128)(2,1)S(1)} %copy-done.2, bf16[64,64,128]{2,0,1:T(8,128)(2,1)} %fusion.35.clone.1.clone.4), kind=kOutput, calls=%fused_computation.38 | convolution fusion | flops 7518945280 | bytes 121241856 | tf_op jit(solution)/shard_map/bhv,hvd->bd/dot_general | solution.py:51
  190.7 0.0 copy-done.9
  190.8 1.2 multiply_convert_fusion
  191.9 0.0 all-gather.2.cloned.1.call-update
  191.9 0.0 reduce-scatter.2.cloned.1.call-start
  192.0 31.4 %all-gather.2.cloned.1.call-done = bf16[256,7168]{1,0:T(8,128)(2,1)} async-done(((bf16[64,7168]{1,0:T(8,128)(2,1)}), bf16[256,7168]{1,0:T(8,128)(2,1)}) %all-gather.2.cloned.1.call-update) | async-done | bytes 3670032 | tf_op jit(solution)/shard_map/all_gather | solution.py:67
  223.4 30.0 %fusion.70 = f32[256,4608]{1,0:T(8,128)} fusion(bf16[256,7168]{1,0:T(8,128)(2,1)} %all-gather.2.cloned.1.call-done, bf16[7168,4608]{1,0:T(8,128)(2,1)} %param.35), kind=kOutput, calls=%fused_computation.76 | convolution fusion | flops 16911433728 | bytes 74448896 | tf_op jit(solution)/shard_map/dot_general | solution.py:68
  253.4 30.0 %fusion.9.clone.4 = bf16[256,4608]{1,0:T(8,128)(2,1)} fusion(bf16[256,7168]{1,0:T(8,128)(2,1)} %all-gather.2.cloned.1.call-done, bf16[7168,4608]{1,0:T(8,128)(2,1)} %param.36, f32[256,4608]{1,0:T(8,128)} %fusion.70), kind=kOutput, calls=%fused_computation.14.clone.clone.clone.1 | convolution fusion | flops 16918511616 | bytes 76808192 | tf_op jit(solution)/shard_map/dot_general | solution.py:69
  283.3 31.1 %fusion.25 = f32[256,7168]{1,0:T(8,128)} fusion(bf16[4608,7168]{1,0:T(8,128)(2,1)} %param.37, bf16[256,4608]{1,0:T(8,128)(2,1)} %fusion.9.clone.4), kind=kOutput, calls=%fused_computation.28 | convolution fusion | flops 16911433728 | bytes 75759616 | tf_op jit(solution)/shard_map/dot_general | solution.py:71
  314.5 0.0 copy-start.8
  314.5 0.0 reduce-scatter.2.cloned.1.call-update
  314.5 0.7 copy-done.8
  315.2 0.7 copy.38
  315.9 56.6 %reduce-scatter.2.cloned.1.call-done = f32[64,7168]{1,0:T(8,128)} async-done(((f32[256,7168]{1,0:T(8,128)}), f32[64,7168]{1,0:T(8,128)}) %reduce-scatter.2.cloned.1.call-update) | async-done | bytes 1835024 | tf_op jit(solution)/shard_map/reduce_scatter | solution.py:72
  372.5 2.6 add_convert_fusion.1
  (7 shorter events, 0.1 us)
Async XLA Ops:
  7.2 216.2 %all-gather.2.cloned.1.call-start = ((), (), s32[]{:S(2)}) async-start(), calls=%async_computation.1 | async-start | bytes 4587520 | tf_op jit(solution)/shard_map/all_gather | solution.py:67
  8.7 6.5 %copy-start.12 = (s32[64]{0:T(128)S(1)}, s32[64]{0:T(128)}, u32[]{:S(2)}) copy-start(s32[64]{0:T(128)} %param.22) | copy-start | bytes 772
  8.7 6.6 %copy-start.7 = (f32[64,32]{0,1:T(8,128)S(1)}, f32[64,32]{0,1:T(8,128)}, u32[]{:S(2)}) copy-start(f32[64,32]{0,1:T(8,128)} %param.23) | copy-start | bytes 24580
  8.7 6.7 %copy-start.6 = (f32[64,32]{0,1:T(8,128)S(1)}, f32[64,32]{0,1:T(8,128)}, u32[]{:S(2)}) copy-start(f32[64,32]{0,1:T(8,128)} %param.24) | copy-start | bytes 24580
  8.7 7.7 %copy-start.2 = (bf16[64,7168]{1,0:T(8,128)(2,1)S(1)}, bf16[64,7168]{1,0:T(8,128)(2,1)}, u32[]{:S(2)}) copy-start(bf16[64,7168]{1,0:T(8,128)(2,1)} %param.19) | copy-start | bytes 2752516
  8.7 7.7 %copy-start.4 = (f32[7168]{0:T(1024)S(1)}, f32[7168]{0:T(1024)}, u32[]{:S(2)}) copy-start(f32[7168]{0:T(1024)} %param.25) | copy-start | bytes 86020
  16.4 9.5 %copy-start.10 = (f32[1536]{0:T(1024)S(1)}, f32[1536]{0:T(1024)}, u32[]{:S(2)}) copy-start(f32[1536]{0:T(1024)} %param.27) | copy-start | bytes 18436
  45.9 21.4 %copy-start = (f32[64,64,192]{2,0,1:T(8,128)S(1)}, f32[64,64,192]{2,0,1:T(8,128)}, u32[]{:S(2)}) copy-start(f32[64,64,192]{2,0,1:T(8,128)} %fusion.53) | copy-start | bytes 9437188
  67.3 8.5 %copy-start.1 = (bf16[64,64,512]{2,0,1:T(8,128)(2,1)}, bf16[64,64,512]{2,0,1:T(8,128)(2,1)S(1)}, u32[]{:S(2)}) copy-start(bf16[64,64,512]{2,0,1:T(8,128)(2,1)S(1)} %convert_bitcast_fusion) | copy-start | bytes 12582916
  67.3 3.7 copy-start.3
  71.0 4.6 %copy-start.11 = (f32[512]{0:T(512)S(1)}, f32[512]{0:T(512)}, u32[]{:S(2)}) copy-start(f32[512]{0:T(512)} %param.30) | copy-start | bytes 6148
  75.8 0.6 copy-start.5
  152.1 38.7 %copy-start.9 = (f32[7168]{0:T(1024)S(1)}, f32[7168]{0:T(1024)}, u32[]{:S(2)}) copy-start(f32[7168]{0:T(1024)} %param.34) | copy-start | bytes 86020
  191.9 180.5 %reduce-scatter.2.cloned.1.call-start = ((), (), s32[]{:S(2)}) async-start(), calls=%async_computation.2 | async-start | bytes 9175040 | tf_op jit(solution)/shard_map/reduce_scatter | solution.py:72
  314.5 0.7 copy-start.8
Sparse Core Ops, SparseCore 0:
  192.1 31.2 all-gather.1
  314.6 57.8 reduce-scatter.1
where the time goes:
time: 387 us; the launch traced here: 382 us
  matrix products  261 us (67%)
  waiting for transfers between devices  88 us (23%)
  other arithmetic  14.7 us (4%)
  between operations  14.7 us (4%)
  local copies, waits for them, and re-layouts  4.06 us (1%)
    reduce_scatter x1, waiting for transfers between devices, local_step(): lax.psum_scatter(partial_sum, 'dp', scatter_dimension=0, tiled=True)  56.6 us
    dot_general x1, matrix products, attention_rows(): jnp.einsum('bhv,hvd->bd', head_out, w_out, preferred_element_type=jnp.flo...  38.7 us
    all_gather x1, waiting for transfers between devices, local_step(): group_in = lax.all_gather(mlp_in, 'dp', axis=0, tiled=True)  31.4 us
    dot_general x1, matrix products, local_step(): partial_sum = jnp.dot(act_val, w_down, preferred_element_type=jnp.float32)  31.1 us
    dot_general x1, matrix products, local_step(): gate_val = jnp.dot(group_in, w_gate, preferred_element_type=jnp.float32)  30 us
    dot_general x1, matrix products, local_step(): up_val = jnp.dot(group_in, w_up, preferred_element_type=jnp.float32)  30 us
    dot_general x1, matrix products, attention_rows(): jnp.einsum('bhl,lhv->bhv', lat_out, w_uv, preferred_element_type=jnp.floa...  24.3 us
    dot_general x1, matrix products, attention_rows(): jnp.einsum('bhl,btl->bht', q_abs, ckv_cache, preferred_element_type=jnp.f...  23.3 us
  transfers between devices with their start and end apart: 2, of which 2 were waited for; matrix products, arithmetic and copies ran while one was open for 0% of the time, Pallas kernels for 0%

commit v1 on v0

--- a/solution.py
+++ b/solution.py
@@ -2,10 +2,13 @@
 import jax
 import jax.numpy as jnp
 from jax import lax
+from jax.experimental import pallas as pl
+from jax.experimental.pallas import tpu as pltpu
 from jax.sharding import PartitionSpec as P
 
 EPSILON = 1e-6
 MSCALE = 0.1 * math.log(40.0) + 1.0
+MESH = pl.DeviceIdType.MESH
 
 
 def rms_norm(values_in, gain_vec):
@@ -21,7 +24,7 @@
     return jnp.concatenate([low_half * cos_t - high_half * sin_t, high_half * cos_t + low_half * sin_t], axis=-1)
 
 
-def attention_rows(hidden, ckv_cache, kpe_cache, cache_len, rope_cos, rope_sin, norm_attn, w_dq, norm_q, w_uq, w_dkv, norm_kv, w_uk, w_uv, w_out):
+def attention_rows(hidden, ckv_cache, kpe_cache, cache_len, rope_cos, rope_sin, norm_attn, w_dq, norm_q, w_uq, w_dkv, norm_kv, w_uk, w_uv):
     nope_dim = w_uk.shape[2]
     value_a7 = w_uk.shape[0]
     score_scale = MSCALE * MSCALE / math.sqrt(w_uq.shape[2])
@@ -48,9 +51,243 @@
                 + exp_new.astype(jnp.bfloat16).astype(jnp.float32)[..., None] * ckv_new.astype(jnp.float32)[:, None, :])
     lat_out = (weighted / norm_sum[..., None]).astype(jnp.bfloat16)
     head_out = jnp.einsum('bhl,lhv->bhv', lat_out, w_uv, preferred_element_type=jnp.float32).astype(jnp.bfloat16)
-    attn_out = jnp.einsum('bhv,hvd->bd', head_out, w_out, preferred_element_type=jnp.float32)
-    residual = (hidden.astype(jnp.float32) + attn_out).astype(jnp.bfloat16)
-    return residual, ckv_new, kpe_new
+    return head_out, ckv_new, kpe_new
+
+
+def _sides():
+    rep = lax.axis_index('rep')
+    me = lax.axis_index('dp')
+    chip = me // 2
+    core = lax.rem(me, 2)
+    return rep, me, chip, core
+
+
+OUT_W = 512
+SLOTS = 4
+
+
+def tail_kernel(o_ref, x_ref, gain_ref, wout_ref, wgate_ref, wup_ref, wdown_ref, out_ref,
+                slots, o_chip, x_chip, r_all, u_all, gate_buf, act, pair_send, pair_recv, far_send, far_recv, own_sum,
+                slot_sem, in_send, in_recv, loc_sem, rp_send, rp_recv, rx_send, rx_recv, rf_send, rf_recv,
+                pp_send, pp_recv, px_send, px_recv):
+    rep, me, chip, core = _sides()
+    part = chip * 2 + (1 - core)
+    opp = (1 - chip) * 2 + core
+    diag = (1 - chip) * 2 + (1 - core)
+    attn_k = wout_ref.shape[0]
+    d_model = wgate_ref.shape[0]
+    ff = wgate_ref.shape[1]
+    rows = x_ref.shape[0]
+    n_out = d_model // 2 // OUT_W
+    n_ff = ff // OUT_W
+    n_down = d_model // OUT_W
+    first_ff = n_out
+    first_down = n_out + 2 * n_ff
+    total = first_down + n_down
+    half = d_model // 2
+
+    def col(index):
+        return pl.ds(pl.multiple_of(index * OUT_W, OUT_W), OUT_W)
+
+    def slot_copy(kind, index, step):
+        slot = lax.rem(step, SLOTS)
+        src = {'out': wout_ref, 'gate': wgate_ref, 'up': wup_ref, 'down': wdown_ref}[kind]
+        depth = src.shape[0]
+        return pltpu.make_async_copy(src.at[:, col(index)], slots.at[slot, pl.ds(0, depth), :], slot_sem.at[slot])
+
+    def fetch(step):
+        @pl.when(step < first_ff)
+        def _():
+            slot_copy('out', core * n_out + step, step).start()
+
+        @pl.when((step >= first_ff) & (step < first_down) & (lax.rem(step - first_ff, 2) == 0))
+        def _():
+            slot_copy('gate', (step - first_ff) // 2, step).start()
+
+        @pl.when((step >= first_ff) & (step < first_down) & (lax.rem(step - first_ff, 2) == 1))
+        def _():
+            slot_copy('up', (step - first_ff) // 2, step).start()
+
+        @pl.when((step >= first_down) & (step < total))
+        def _():
+            slot_copy('down', step - first_down, step).start()
+
+    for step in range(SLOTS - 1):
+        slot_copy('out', core * n_out + step, step).start()
+
+    barrier = pltpu.get_barrier_semaphore()
+    for peer in (part, opp):
+        pl.semaphore_signal(barrier, inc=1, device_id=(rep, peer), device_id_type=MESH)
+    pl.semaphore_wait(barrier, 2)
+
+    def remote(src, dst, send, recv, peer):
+        return pltpu.make_async_remote_copy(src_ref=src, dst_ref=dst, send_sem=send, recv_sem=recv,
+                                            device_id=(rep, peer), device_id_type=MESH)
+
+    my_rows = pl.ds(pl.multiple_of(core * rows, rows), rows)
+    send_o = remote(o_ref, o_chip.at[my_rows, :], in_send.at[0], in_recv.at[0], part)
+    send_o.start()
+    their_half = pl.ds(pl.multiple_of((1 - core) * half, half), half)
+    send_x = remote(x_ref.at[:, their_half], x_chip.at[my_rows, :], in_send.at[1], in_recv.at[1], part)
+    send_x.start()
+    my_half = pl.ds(pl.multiple_of(core * half, half), half)
+    keep_o = pltpu.make_async_copy(o_ref, o_chip.at[my_rows, :], loc_sem.at[0])
+    keep_o.start()
+    keep_x = pltpu.make_async_copy(x_ref.at[:, my_half], x_chip.at[my_rows, :], loc_sem.at[1])
+    keep_x.start()
+    keep_o.wait()
+    keep_x.wait()
+    send_o.wait()
+    send_x.wait()
+
+    chip_rows = pl.ds(pl.multiple_of(chip * 2 * rows, 2 * rows), 2 * rows)
+    far_rows = pl.ds(pl.multiple_of((1 - chip) * 2 * rows, 2 * rows), 2 * rows)
+
+    def r_pair(index):
+        blk = r_all.at[core * n_out + index, chip_rows, :]
+        return remote(blk, blk, rp_send.at[index], rp_recv.at[index], part)
+
+    def r_far(index):
+        blk = r_all.at[core * n_out + index, chip_rows, :]
+        return remote(blk, blk, rx_send.at[index], rx_recv.at[index], opp)
+
+    def r_forward(index):
+        blk = r_all.at[core * n_out + index, far_rows, :]
+        return remote(blk, blk, rf_send.at[index], rf_recv.at[index], part)
+
+    def forward(index):
+        r_far(index).wait_recv()
+        r_forward(index).start()
+
+    def out_step(index, carry):
+        fetch(index + SLOTS - 1)
+        slot_copy('out', core * n_out + index, index).wait()
+        acc = jnp.dot(o_chip[...], slots[lax.rem(index, SLOTS), :attn_k, :], preferred_element_type=jnp.float32)
+        r_all[core * n_out + index, chip_rows, :] = (x_chip[:, col(index)].astype(jnp.float32) + acc).astype(jnp.bfloat16)
+        r_far(index).start()
+        r_pair(index).start()
+
+        @pl.when(index >= 2)
+        def _():
+            forward(index - 2)
+        return carry
+
+    lax.fori_loop(0, n_out, out_step, 0)
+    for index in range(n_out - 2, n_out):
+        forward(index)
+    for index in range(n_out):
+        r_pair(index).wait()
+        r_far(index).wait_send()
+        r_forward(index).wait()
+
+    def square_step(index, total_sq):
+        vals = r_all[index].astype(jnp.float32)
+        return total_sq + jnp.sum(vals * vals, axis=-1, keepdims=True)
+
+    total_sq = lax.fori_loop(0, n_down, square_step, jnp.zeros((4 * rows, 1), jnp.float32))
+    gate_buf[:, 0:1] = lax.rsqrt(total_sq * (1.0 / d_model) + EPSILON)
+    order = (part, diag, me, opp)
+
+    def norm_step(index, carry):
+        for place, owner in enumerate(order):
+            src = pl.ds(pl.multiple_of(owner * rows, rows), rows)
+            vals = r_all[index, src, :].astype(jnp.float32) * gate_buf[src, 0:1] * gain_ref[0:1, col(index)]
+            u_all[place * rows:(place + 1) * rows, col(index)] = vals.astype(jnp.bfloat16)
+        return carry
+
+    lax.fori_loop(0, n_down, norm_step, 0)
+
+    def ff_step(index, carry):
+        step = first_ff + 2 * index
+        fetch(step + SLOTS - 1)
+        slot_copy('gate', index, step).wait()
+        gate_buf[...] = jnp.dot(u_all[...], slots[lax.rem(step, SLOTS), :d_model, :], preferred_element_type=jnp.float32)
+        fetch(step + SLOTS)
+        slot_copy('up', index, step + 1).wait()
+        up_val = jnp.dot(u_all[...], slots[lax.rem(step + 1, SLOTS), :d_model, :], preferred_element_type=jnp.float32)
+        gate_val = gate_buf[...]
+        act[:, col(index)] = (gate_val * jax.nn.sigmoid(gate_val) * up_val).astype(jnp.bfloat16)
+        return carry
+
+    lax.fori_loop(0, n_ff, ff_step, 0)
+
+    def pair_copy(index):
+        return remote(pair_send.at[index], pair_recv.at[index], pp_send.at[index], pp_recv.at[index], part)
+
+    def far_copy(index):
+        return remote(far_send.at[index], far_recv.at[index], px_send.at[index], px_recv.at[index], opp)
+
+    def combine(index):
+        pair_copy(index).wait_recv()
+        far_send[index] += pair_recv[index, rows:, :]
+        far_copy(index).start()
+        own_sum[index] += pair_recv[index, :rows, :]
+
+    def down_step(index, carry):
+        step = first_down + index
+        fetch(step + SLOTS - 1)
+        slot_copy('down', index, step).wait()
+        part_sum = jnp.dot(act[...], slots[lax.rem(step, SLOTS), :ff, :], preferred_element_type=jnp.float32)
+        pair_send[index] = part_sum[:2 * rows]
+        own_sum[index] = part_sum[2 * rows:3 * rows]
+        far_send[index] = part_sum[3 * rows:]
+        pair_copy(index).start()
+
+        @pl.when(index >= 1)
+        def _():
+            combine(index - 1)
+        return carry
+
+    lax.fori_loop(0, n_down, down_step, 0)
+    combine(n_down - 1)
+    own_rows = pl.ds(pl.multiple_of(me * rows, rows), rows)
+
+    def finish(index, carry):
+        far_copy(index).wait()
+        pair_copy(index).wait_send()
+        mlp = own_sum[index] + far_recv[index]
+        out_ref[:, col(index)] = (r_all[index, own_rows, :].astype(jnp.float32) + mlp).astype(jnp.bfloat16)
+        return carry
+
+    lax.fori_loop(0, n_down, finish, 0)
+
+
+def tail(head_out, hidden, norm_mlp, w_out, w_gate, w_up, w_down):
+    rows, d_model = hidden.shape
+    attn_k = w_out.shape[0]
+    ff = w_gate.shape[1]
+    n_out = d_model // 2 // OUT_W
+    n_down = d_model // OUT_W
+    depth = max(attn_k, d_model, ff)
+    vmem = pl.BlockSpec(memory_space=pltpu.VMEM)
+    anywhere = pl.BlockSpec(memory_space=pl.ANY)
+    dma = pltpu.SemaphoreType.DMA
+    f32, bf16 = jnp.float32, jnp.bfloat16
+    return pl.pallas_call(
+        tail_kernel,
+        out_shape=jax.ShapeDtypeStruct((rows, d_model), bf16),
+        in_specs=[vmem, vmem, vmem, anywhere, anywhere, anywhere, anywhere],
+        out_specs=vmem,
+        scratch_shapes=[
+            pltpu.VMEM((SLOTS, depth, OUT_W), bf16),
+            pltpu.VMEM((2 * rows, attn_k), bf16),
+            pltpu.VMEM((2 * rows, d_model // 2), bf16),
+            pltpu.VMEM((n_down, 4 * rows, OUT_W), bf16),
+            pltpu.VMEM((4 * rows, d_model), bf16),
+            pltpu.VMEM((4 * rows, OUT_W), f32),
+            pltpu.VMEM((4 * rows, ff), bf16),
+            pltpu.VMEM((n_down, 2 * rows, OUT_W), f32),
+            pltpu.VMEM((n_down, 2 * rows, OUT_W), f32),
+            pltpu.VMEM((n_down, rows, OUT_W), f32),
+            pltpu.VMEM((n_down, rows, OUT_W), f32),
+            pltpu.VMEM((n_down, rows, OUT_W), f32),
+            dma((SLOTS,)), dma((2,)), dma((2,)), dma((2,)),
+            dma((n_out,)), dma((n_out,)), dma((n_out,)), dma((n_out,)), dma((n_out,)), dma((n_out,)),
+            dma((n_down,)), dma((n_down,)), dma((n_down,)), dma((n_down,)),
+        ],
+        compiler_params=pltpu.CompilerParams(collective_id=0, has_side_effects=True, vmem_limit_bytes=66 * 1000 * 1000),
+        name='tail',
+    )(head_out, hidden, norm_mlp.reshape(1, d_model), w_out, w_gate, w_up, w_down)
 
 
 def solution(mesh):
@@ -62,15 +299,8 @@
                 P(None, 'dp'), P(None, 'dp'), P('dp', None))
 
     def local_step(hidden, ckv_cache, kpe_cache, cache_len, rope_cos, rope_sin, norm_attn, w_dq, norm_q, w_uq, w_dkv, norm_kv, w_uk, w_uv, w_out, norm_mlp, w_gate, w_up, w_down):
-        residual, ckv_new, kpe_new = attention_rows(hidden, ckv_cache, kpe_cache, cache_len, rope_cos, rope_sin, norm_attn, w_dq, norm_q, w_uq, w_dkv, norm_kv, w_uk, w_uv, w_out)
-        mlp_in = rms_norm(residual, norm_mlp).astype(jnp.bfloat16)
-        group_in = lax.all_gather(mlp_in, 'dp', axis=0, tiled=True)
-        gate_val = jnp.dot(group_in, w_gate, preferred_element_type=jnp.float32)
-        up_val = jnp.dot(group_in, w_up, preferred_element_type=jnp.float32)
-        act_val = (jax.nn.silu(gate_val) * up_val).astype(jnp.bfloat16)
-        partial_sum = jnp.dot(act_val, w_down, preferred_element_type=jnp.float32)
-        mlp_rows = lax.psum_scatter(partial_sum, 'dp', scatter_dimension=0, tiled=True)
-        out_hidden = (residual.astype(jnp.float32) + mlp_rows).astype(jnp.bfloat16)
+        head_out, ckv_new, kpe_new = attention_rows(hidden, ckv_cache, kpe_cache, cache_len, rope_cos, rope_sin, norm_attn, w_dq, norm_q, w_uq, w_dkv, norm_kv, w_uk, w_uv)
+        out_hidden = tail(head_out.reshape(hidden.shape[0], -1), hidden, norm_mlp, w_out.reshape(-1, w_out.shape[-1]), w_gate, w_up, w_down)
         return out_hidden, ckv_new, kpe_new
 
     return jax.shard_map(local_step, mesh=mesh, in_specs=in_specs, out_specs=(row_spec, row_spec, row_spec), check_vma=False)

time: 387 us -> 264 us (0.68)
  matrix products: 261 us -> 120 us
  Pallas kernels: 0 us -> 119 us
  waiting for transfers between devices: 88 us -> 0 us
  between operations: 14.7 us -> 1.13 us
    dot_general x4 -> x0, matrix products: 130 us -> none  [the longest x1 38.7 us: attention_rows(): jnp.einsum('bhv,hvd->bd', head_out, w_out, preferred_element_type=jnp.flo...]
    pallas_call x0 -> x1, Pallas kernels: none -> 119 us  [tail(): pl.pallas_call(tail_kernel, out_shape=jax.ShapeDtypeStruct((rows, d_model...]
    reduce_scatter x1 -> x0, waiting for transfers between devices: 56.6 us -> none  [local_step(): lax.psum_scatter(partial_sum, 'dp', scatter_dimension=0, tiled=True)]
    all_gather x1 -> x0, waiting for transfers between devices: 31.4 us -> none  [local_step(): group_in = lax.all_gather(mlp_in, 'dp', axis=0, tiled=True)]
    dot_general x1, matrix products: 24.3 us -> 13.9 us  [attention_rows(): jnp.einsum('bhl,lhv->bhv', lat_out, w_uv, preferred_element_type=jnp.floa...]
  transfers between devices with their start and end apart: 2 -> 0, of which waited for: 2 -> 0; matrix products, arithmetic and copies ran while one was open for 0% -> 0% of each run, Pallas kernels for 0% -> 0%
where the time goes in v1:
time: 264 us; the launch traced here: 259 us
  matrix products  120 us (45%)
  Pallas kernels  119 us (45%)
  other arithmetic  13.4 us (5%)
  local copies, waits for them, and re-layouts  5.38 us (2%)
    pallas_call x1, Pallas kernels, tail(): pl.pallas_call(tail_kernel, out_shape=jax.ShapeDtypeStruct((rows, d_model...  119 us
    dot_general x1, matrix products, attention_rows(): jnp.einsum('bhl,btl->bht', q_abs, ckv_cache, preferred_element_type=jnp.f...  23.3 us
    dot_general x1, matrix products, attention_rows(): jnp.einsum('bl,lhe->bhe', q_latent, w_uq, preferred_element_type=jnp.floa...  20 us
    dot_general x1, matrix products, attention_rows(): jnp.einsum('bhn,lhn->bhl', q_nope, w_uk, preferred_element_type=jnp.float32)  19.2 us
    dot_general x1, matrix products, attention_rows(): jnp.einsum('bht,btl->bhl', exp_cache.astype(jnp.bfloat16), ckv_cache, pre...  18.3 us
    dot_general x1, matrix products, attention_rows(): jnp.einsum('bhl,lhv->bhv', lat_out, w_uv, preferred_element_type=jnp.floa...  13.9 us
    dot_general x1, matrix products, attention_rows(): jnp.dot(normed, w_dq, preferred_element_type=jnp.float32)  9.48 us
    reduce_sum x1, other arithmetic, attention_rows(): norm_sum = jnp.sum(exp_cache, axis=-1) + exp_new  7.2 us

profile of v1, /device:TPU:0, one launch (start us, length us, event | category | flops | bytes accessed | tf_op | source)
XLA Modules:
  0.0 259.2 jit_solution(12327462312820016020)
XLA Ops:
  0.6 0.0 copy-start.1
  0.6 0.0 copy-start.5
  0.7 0.0 copy-start.7
  0.7 0.0 copy-start.8
  0.7 1.5 fusion.24
  2.2 6.2 %fusion.41 = f32[64,576]{1,0:T(8,128)S(1)} fusion(bf16[7168,576]{0,1:T(8,128)(2,1)} %param.29, bf16[64,7168]{1,0:T(8,128)(2,1)} %x_ref.1, f32[7168]{0:T(1024)} %param.25, f32[64]{0:T(128)S(1)} %add_rsqrt_fusion.2), kind=kOutput, calls=%fused_computation.42 | convolution fusion | flops 530317312 | bytes 9351424 | tf_op jit(solution)/shard_map/dot_general | solution.py:36
  8.5 0.0 copy-start.3
  8.5 0.7 copy-done.3
  9.1 0.1 fusion.57
  9.2 0.1 copy.52
  9.3 0.1 copy.53
  9.3 0.0 copy-done.7
  9.4 0.0 copy-done.8
  9.4 0.6 pad_maximum_fusion.1
  10.0 0.1 copy.49
  10.1 0.0 copy-done.1
  10.1 0.0 copy-done.5
  10.1 0.0 copy-start.10
  10.1 9.5 %multiply_reduce_fusion = (f32[64]{0:T(128)S(1)}, f32[64,1536]{1,0:T(8,128)S(1)}) fusion(bf16[7168,1536]{1,0:T(8,128)(2,1)} %param.26, bf16[64,7168]{1,0:T(8,128)(2,1)S(1)} %copy-done.1, f32[7168]{0:T(1024)S(1)} %copy-done.5, f32[64]{0:T(128)S(1)} %add_rsqrt_fusion.2), kind=kOutput, calls=%fused_computation.41 | convolution fusion | flops 1411317760 | bytes 23360000 | tf_op jit(solution)/shard_map/dot_general | solution.py:32
  19.6 0.0 copy-done.10
  19.6 20.0 %fusion.46 = f32[64,64,192]{2,0,1:T(8,128)} fusion(bf16[1536,64,192]{0,2,1:T(8,128)(2,1)} %param.28, f32[64,1536]{1,0:T(8,128)S(1)} %get-tuple-element.19, f32[1536]{0:T(1024)S(1)} %copy-done.10, f32[64]{0:T(128)S(1)} %add_rsqrt_fusion.1), kind=kOutput, calls=%fused_computation.45 | convolution fusion | flops 2416214016 | bytes 41294080 | tf_op jit(solution)/shard_map/bl,lhe->bhe/dot_general | solution.py:33
  39.6 0.1 copy.37
  39.7 0.1 copy.38
  39.8 0.0 copy-start.2
  39.8 0.0 slice-start
  39.8 3.2 %subtract_convert_fusion = (bf16[64,64,32]{2,0,1:T(8,128)(2,1)S(1)}, bf16[64,64,32]{2,0,1:T(8,128)(2,1)S(1)}) fusion(f32[64,64,192]{2,0,1:T(8,128)} %fusion.46, f32[64,32]{1,0:T(8,128)S(1)} %copy.38, f32[64,32]{1,0:T(8,128)S(1)} %copy.37), kind=kLoop, calls=%fused_computation.28 | loop fusion | flops 1048576 | bytes 1589248 | tf_op jit(solution)/shard_map/convert.2
  43.0 0.0 copy-start
  43.0 0.6 pad_maximum_fusion
  43.6 0.8 fusion.37
  44.4 0.0 copy-done.2
  44.4 0.0 slice-start.1
  44.4 4.7 %fusion.39 = f32[64,64,512]{2,1,0:T(8,128)} fusion(bf16[64,512,64]{1,2,0:T(8,128)(2,1)S(1)} %copy-done.2, bf16[64,64,64]{2,0,1:T(8,128)(2,1)S(1)} %pad_maximum_fusion), kind=kOutput, calls=%fused_computation.38 | convolution fusion | flops 268435456 | bytes 13107200 | tf_op jit(solution)/shard_map/bhr,btr->bht/dot_general | solution.py:41
  49.1 0.0 slice-done
  49.1 0.0 copy-done
  49.1 0.0 slice-done.1
  49.1 0.0 copy-start.12
  49.1 19.2 %convert_bitcast_fusion = bf16[64,64,512]{2,0,1:T(8,128)(2,1)} fusion(bf16[512,64,128]{2,1,0:T(8,128)(2,1)S(1)} %bitcast.28, f32[64,64,192]{2,0,1:T(8,128)S(1)} %copy-done), kind=kOutput, calls=%fused_computation.18 | convolution fusion | flops 538968064 | bytes 13631488 | tf_op jit(solution)/shard_map/bhn,lhn->bhl/dot_general | solution.py:39
  68.3 0.0 copy-done.12
  68.3 0.1 iota_compare_fusion
  68.4 0.0 copy-start.4
  68.4 0.0 copy-start.11
  68.4 23.3 %fusion.15 = (f32[64,64]{1,0:T(8,128)S(1)}, f32[64,64,512]{2,1,0:T(8,128)}) fusion(f32[64,64,512]{2,1,0:T(8,128)} %fusion.39, pred[64,512]{1,0:T(8,128)(4,1)S(1)} %iota_compare_fusion, bf16[64,512,512]{2,1,0:T(8,128)(2,1)} %param.20, bf16[64,64,512]{2,0,1:T(8,128)(2,1)} %convert_bitcast_fusion), kind=kOutput, calls=%fused_computation.16 | convolution fusion | flops 2155868160 | bytes 54575104 | tf_op jit(solution)/shard_map/bhl,btl->bht/dot_general | solution.py:40
  91.7 0.0 copy-done.4
  91.7 0.1 multiply_reduce_fusion.1
  91.8 0.0 copy-done.11
  91.8 0.1 fusion.56
  91.9 0.0 copy-start.6
  91.9 4.5 %fusion.18 = f32[64,1,64]{2,1,0:T(1,128)S(1)} fusion(bf16[64,64,512]{2,0,1:T(8,128)(2,1)} %convert_bitcast_fusion, bf16[64,512,1]{1,0,2:T(8,128)(2,1)S(1)} %bitcast.34), kind=kOutput, calls=%fused_computation.20 | convolution fusion | flops 4194304 | bytes 4276224 | tf_op jit(solution)/shard_map/bhl,bl->bh/dot_general | solution.py:44
  96.5 7.2 %fusion.6 = f32[64,64]{1,0:T(8,128)S(1)} fusion(f32[64,64]{1,0:T(8,128)S(1)} %fusion.51, f32[64,64,512]{2,1,0:T(8,128)} %get-tuple-element.21, f32[64,64,512]{2,1,0:T(8,128)} %fusion.39, pred[64,512]{1,0:T(8,128)(4,1)S(1)} %iota_compare_fusion), kind=kLoop, calls=%fused_computation.9 | loop fusion | flops 10481664 | bytes 16842752 | tf_op jit(solution)/shard_map/reduce_sum | solution.py:49
  103.7 0.0 copy-done.6
  103.8 0.1 copy.42
  103.8 0.1 copy.43
  103.9 18.3 %fusion.9 = f32[64,64,512]{2,1,0:T(8,128)S(1)} fusion(bf16[64,512,512]{2,1,0:T(8,128)(2,1)} %param.20, f32[64,64]{1,0:T(8,128)S(1)} %fusion.51, f32[64,64,512]{2,1,0:T(8,128)} %get-tuple-element.21, f32[64,64,512]{2,1,0:T(8,128)} %fusion.39, pred[64,512]{1,0:T(8,128)(4,1)S(1)} %iota_compare_fusion), kind=kOutput, calls=%fused_computation.11 | convolution fusion | flops 2157969408 | bytes 58769408 | tf_op jit(solution)/shard_map/bht,btl->bhl/dot_general | solution.py:50
  122.3 13.9 %fusion.32 = bf16[64,8,8,128]{3,2,1,0:T(8,128)(2,1)S(1)} fusion(bf16[512,64,128]{2,1,0:T(8,128)(2,1)} %param.32, f32[64,64,512]{2,1,0:T(8,128)S(1)} %fusion.9, f32[64,64]{0,1:T(8,128)S(1)} %copy.43, f32[64,512]{1,0:T(8,128)S(1)} %get-tuple-element.6, f32[64,64]{0,1:T(8,128)S(1)} %copy.42), kind=kOutput, calls=%fused_computation.33 | convolution fusion | flops 545783808 | bytes 17989632 | tf_op jit(solution)/shard_map/bhl,lhv->bhv/dot_general | solution.py:53
  136.2 1.2 copy.88
  137.4 0.0 copy-start.9
  137.4 118.8 %tail.1 = bf16[64,7168]{1,0:T(8,128)(2,1)} custom-call(bf16[64,8192]{1,0:T(8,128)(2,1)} %bitcast.29, bf16[64,7168]{1,0:T(8,128)(2,1)} %x_ref.1, f32[1,7168]{1,0:T(1,128)} %bitcast.35, bf16[8192,7168]{1,0:T(8,128)(2,1)} %bitcast.10.wout_ref, bf16[7168,4608]{1,0:T(8,128)(2,1)} %wgate_ref.1, bf16[7168,4608]{1,0:T(8,128)(2,1)} %wup_ref.1, ...), custom_call_target="tpu_custom_call" | custom-call | tf_op jit(solution)/shard_map/tail/pallas_call | solution.py:266
  256.2 0.0 copy-done.9
  256.2 0.7 copy.46
  256.9 2.2 copy.90
  (7 shorter events, 0.1 us)
Async XLA Ops:
  0.6 9.5 %copy-start.1 = (bf16[64,7168]{1,0:T(8,128)(2,1)S(1)}, bf16[64,7168]{1,0:T(8,128)(2,1)}, u32[]{:S(2)}) copy-start(bf16[64,7168]{1,0:T(8,128)(2,1)} %x_ref.1) | copy-start | bytes 2752516
  0.6 9.5 %copy-start.5 = (f32[7168]{0:T(1024)S(1)}, f32[7168]{0:T(1024)}, u32[]{:S(2)}) copy-start(f32[7168]{0:T(1024)} %param.25) | copy-start | bytes 86020
  0.7 8.7 %copy-start.7 = (f32[64,32]{0,1:T(8,128)S(1)}, f32[64,32]{0,1:T(8,128)}, u32[]{:S(2)}) copy-start(f32[64,32]{0,1:T(8,128)} %param.23) | copy-start | bytes 24580
  0.7 8.7 %copy-start.8 = (f32[64,32]{0,1:T(8,128)S(1)}, f32[64,32]{0,1:T(8,128)}, u32[]{:S(2)}) copy-start(f32[64,32]{0,1:T(8,128)} %param.24) | copy-start | bytes 24580
  8.5 0.7 copy-start.3
  10.1 9.5 %copy-start.10 = (f32[1536]{0:T(1024)S(1)}, f32[1536]{0:T(1024)}, u32[]{:S(2)}) copy-start(f32[1536]{0:T(1024)} %param.27) | copy-start | bytes 18436
  39.8 4.6 %copy-start.2 = (bf16[64,512,64]{1,2,0:T(8,128)(2,1)S(1)}, bf16[64,512,64]{1,2,0:T(8,128)(2,1)}, u32[]{:S(2)}) copy-start(bf16[64,512,64]{1,2,0:T(8,128)(2,1)} %param.21) | copy-start | bytes 12582916
  39.8 9.3 %slice-start = ((s8[8388608]{0:T(1024)(128)(4,1)}), s8[4194304]{0:T(1024)(128)(4,1)S(1)}, s32[]{:S(2)}) async-start(s8[8388608]{0:T(1024)(128)(4,1)} %bitcast.27), calls=%async_computation | async-start | bytes 8388608
  43.0 6.1 %copy-start = (f32[64,64,192]{2,0,1:T(8,128)S(1)}, f32[64,64,192]{2,0,1:T(8,128)}, u32[]{:S(2)}) copy-start(f32[64,64,192]{2,0,1:T(8,128)} %fusion.46) | copy-start | bytes 9437188
  44.4 4.7 %slice-start.1 = ((s8[8388608]{0:T(1024)(128)(4,1)}), s8[4194304]{0:T(1024)(128)(4,1)S(1)}, s32[]{:S(2)}) async-start(s8[8388608]{0:T(1024)(128)(4,1)} %bitcast.27), calls=%async_computation.1 | async-start | bytes 8388608
  49.1 19.2 %copy-start.12 = (s32[64]{0:T(128)S(1)}, s32[64]{0:T(128)}, u32[]{:S(2)}) copy-start(s32[64]{0:T(128)} %param.22) | copy-start | bytes 772
  68.4 23.3 %copy-start.4 = (f32[64,576]{1,0:T(8,128)S(1)}, f32[64,576]{1,0:T(8,128)}, u32[]{:S(2)}) copy-start(f32[64,576]{1,0:T(8,128)} %copy-done.3) | copy-start | bytes 442372
  68.4 23.4 %copy-start.11 = (f32[512]{0:T(512)S(1)}, f32[512]{0:T(512)}, u32[]{:S(2)}) copy-start(f32[512]{0:T(512)} %param.30) | copy-start | bytes 6148
  91.9 11.8 %copy-start.6 = (bf16[64,512]{1,0:T(8,128)(2,1)}, bf16[64,512]{1,0:T(8,128)(2,1)S(1)}, u32[]{:S(2)}) copy-start(bf16[64,512]{1,0:T(8,128)(2,1)S(1)} %get-tuple-element.26) | copy-start | bytes 196612
  137.4 118.8 %copy-start.9 = (bf16[64,64]{0,1:T(8,128)(2,1)S(1)}, bf16[64,64]{0,1:T(8,128)(2,1)}, u32[]{:S(2)}) copy-start(bf16[64,64]{0,1:T(8,128)(2,1)} %get-tuple-element.16) | copy-start | bytes 24580
